TPU v7x, 32 devices: a whole 2x2x4 slice. The times are simulated.
32 devices in a mesh: dp: 4 (over z), vocab: 8 (over y, x, core).
Axes of the slice: x: 2, y: 2, z: 4, core: 2. Of those that a mesh axis runs over, the one named last changes fastest.
Arguments:
- hidden: bfloat16 [512, 4096], P(('dp', 'vocab')), may hold values from -64 to 64
- head_weight: bfloat16 [4096, 128256], P(None, ('dp', 'vocab')), may hold values from -0.0625 to 0.0625
- targets: int32 [512], P(('dp', 'vocab')), may hold values from 0 to 128255
- bench_ids: int32 [512], P(('dp', 'vocab')), may hold values from 0 to 39, as said below
- valid: int32 [512], P(('dp', 'vocab')), may hold values from 0 to 1, as said below
- seq_lengths: int32 [16], replicated, may hold values from 1 to 64, 512 in all
Outputs:
- token_loss: float32 [512], P(('dp', 'vocab'))
- bench_loss: float32 [40], replicated
- bench_count: float32 [40], replicated
Inputs may be any that keep to these rules, and one draw needn't show every extreme that they name: `valid`: among the 16 positions of one device (aligned blocks) at most 8 have validity 1, and some block has exactly 8. `bench_ids`: A benchmark may have no positions in the window.
All inputs are finite; a program needn't handle non-finite values.
Results may differ from a plain program's by a relative error of at most 0.0003.
Values may be sent and summed in bfloat16 or wider, within the bound.
A program may use at most 128 MiB of HBM per device.

v0:
```python
import jax
import jax.numpy as jnp
from jax import lax
from jax.sharding import PartitionSpec as P

BENCH = 40


def body(hidden, head_weight, targets, bench_ids, valid, seq_lengths):
    row_count = hidden.shape[0]
    col_width = head_weight.shape[1]
    device_index = lax.axis_index(("dp", "vocab"))
    col_offset = device_index * col_width
    seq_ends = jnp.cumsum(seq_lengths) - 1
    positions = device_index * row_count + jnp.arange(row_count, dtype=jnp.int32)
    is_end = jnp.any(positions[:, None] == seq_ends[None, :], axis=1)
    scored = valid * (1 - is_end.astype(jnp.int32))
    scored_float = scored.astype(jnp.float32)
    labels = jnp.stack([targets, bench_ids, scored], axis=1)
    gathered_rows = row_count * lax.axis_size(("dp", "vocab"))
    column_ids = jnp.arange(col_width, dtype=jnp.int32)
    empty = jnp.zeros((gathered_rows,), jnp.float32)
    empty_labels = jnp.zeros((gathered_rows, 3), jnp.int32)
    block_rows = lax.all_gather(hidden, ("dp", "vocab"), axis=0, tiled=True)
    block_labels = lax.all_gather(labels, ("dp", "vocab"), axis=0, tiled=True)
    logits = jnp.dot(block_rows, head_weight, preferred_element_type=jnp.float32)
    row_top = jnp.max(logits, axis=1)
    row_total = jnp.sum(jnp.exp(logits - row_top[:, None]), axis=1)
    local_ids = block_labels[:, 0] - col_offset
    hits = column_ids[None, :] == local_ids[:, None]
    target_logit = jnp.sum(jnp.where(hits, logits, 0.0), axis=1)
    row_top, row_total, target_logit, all_labels = (
        row_top,
        row_total,
        target_logit,
        lax.dynamic_update_slice_in_dim(
            (empty, empty, empty, empty_labels)[3], block_labels, jnp.int32(0), 0
        ),
    )
    best = lax.pmax(row_top, ("dp", "vocab"))
    summed, target_sum = lax.psum(
        (row_total * jnp.exp(row_top - best), target_logit), ("dp", "vocab")
    )
    all_losses = best + jnp.log(summed) - target_sum
    own_losses = lax.dynamic_slice_in_dim(all_losses, device_index * row_count, row_count)
    token_loss = own_losses * scored_float
    bench_range = jnp.arange(BENCH, dtype=jnp.int32)
    scored_all = all_labels[:, 2].astype(jnp.float32)
    onehot_all = (all_labels[:, 1][:, None] == bench_range[None, :]).astype(jnp.float32)
    loss_sums = jnp.sum(onehot_all * (all_losses * scored_all)[:, None], axis=0)
    token_counts = jnp.sum(onehot_all * scored_all[:, None], axis=0)
    bench_loss = loss_sums / jnp.maximum(token_counts, 1.0)
    return (token_loss, bench_loss, token_counts)


def solution(mesh):
    placed = (
        P(("dp", "vocab"), None),
        P(None, ("dp", "vocab")),
        P(("dp", "vocab")),
        P(("dp", "vocab")),
        P(("dp", "vocab")),
        P(),
    )
    return jax.shard_map(
        body, mesh=mesh, in_specs=placed, out_specs=(P(("dp", "vocab")), P(), P()), check_vma=False
    )
```

profile of v0, /device:TPU:0, one launch (start us, length us, event | category | flops | bytes accessed | tf_op | source)
XLA Modules:
  0.0 190.8 jit_solution(16473174855132264849)
XLA Ops:
  7.2 0.0 all-gather.3.cloned.1.call-start
  7.2 0.7 all-gather.3.cloned.1.call-update
  7.9 0.7 copy.14
  8.7 0.1 add_reduce_fusion
  8.8 0.2 compare_reduce_fusion
  9.0 0.7 fusion
  9.6 0.7 add_bitcast_fusion
  10.3 43.7 %all-gather = s32[32,16,3]{1,2,0:T(4,128)S(1)} all-gather(s32[1,16,3]{1,2,0:T(4,128)S(1)} %add_bitcast_fusion), channel_id=1, replica_groups=mesh['dp'=4,'vocab'=8] {'dp','vocab'}, dimensions={0}, use_global_device_ids=true | all-gather | bytes 6336 | tf_op jit(solution)/shard_map/all_gather | solution.py:25
  54.0 0.1 reshape.42
  54.1 21.3 %all-gather.3.cloned.1.call-done = bf16[512,4096]{1,0:T(8,128)(2,1)} async-done(((bf16[16,4096]{1,0:T(8,128)(2,1)}), bf16[512,4096]{1,0:T(8,128)(2,1)}) %all-gather.3.cloned.1.call-update) | async-done | bytes 4194320 | tf_op jit(solution)/shard_map/all_gather | solution.py:24
  75.4 23.7 %fusion.3 = (f32[512]{0:T(512)S(1)}, f32[512,4008]{0,1:T(8,128)}) fusion(bf16[512,4096]{1,0:T(8,128)(2,1)} %all-gather.3.cloned.1.call-done, bf16[4096,4008]{0,1:T(8,128)(2,1)} %param.7), kind=kOutput, calls=%fused_computation.20 | convolution fusion | flops 16812822528 | bytes 45238272 | tf_op jit(solution)/shard_map/dot_general | solution.py:26
  99.1 0.0 copy-start.1
  99.1 39.1 %pmax.7 = f32[512]{0:T(512)S(1)} all-reduce(f32[512]{0:T(512)S(1)} %get-tuple-element.14), channel_id=1, replica_groups=mesh['dp'=4,'vocab'=8] {'dp','vocab'}, use_global_device_ids=true, to_apply=%region_1.2 | all-reduce | flops 512 | bytes 4096 | tf_op jit(solution)/shard_map/pmax | solution.py:40
  138.2 4.5 %exponential_reduce_fusion = (f32[512]{0:T(512)S(1)}, f32[512]{0:T(512)S(1)}) fusion(f32[512,4008]{0,1:T(8,128)} %get-tuple-element.15, f32[512]{0:T(512)S(1)} %get-tuple-element.14, s32[512]{0:T(512)S(1)} %bitcast.16), kind=kLoop, calls=%fused_computation.2 | loop fusion | flops 10259456 | bytes 8216576 | tf_op jit(solution)/shard_map/reduce_sum | solution.py:28
  142.7 40.0 %all-reduce = (f32[512]{0:T(512)S(1)}, f32[512]{0:T(512)S(1)}) all-reduce(f32[512]{0:T(512)S(1)} %get-tuple-element.4, f32[512]{0:T(512)S(1)} %exponential_multiply_fusion), channel_id=1, replica_groups=mesh['dp'=4,'vocab'=8] {'dp','vocab'}, use_global_device_ids=true, to_apply=%region_7.8 | all-reduce | flops 1024 | bytes 8192 | tf_op jit(solution)/shard_map/psum | solution.py:41
  182.7 0.0 copy-done.1
  182.7 0.6 convert_multiply_fusion
  183.3 0.1 select_reduce_fusion.1
  183.4 0.0 copy-start
  183.4 0.5 maximum_divide_fusion
  183.9 0.0 copy-done
  (6 shorter events, 0.1 us)
Async XLA Ops:
  7.2 68.2 %all-gather.3.cloned.1.call-start = ((), (), s32[]{:S(2)}) async-start(), calls=%async_computation | async-start | bytes 4325376 | tf_op jit(solution)/shard_map/all_gather | solution.py:24
  99.1 83.6 %copy-start.1 = (s32[16]{0:T(128)S(1)}, s32[16]{0:T(128)}, u32[]{:S(2)}) copy-start(s32[16]{0:T(128)} %param.10) | copy-start | bytes 196
  183.4 0.5 copy-start
Sparse Core Ops, SparseCore 0:
  10.8 64.4 all-gather.2
where the time goes:
time: 191 us
  blocking collectives  123 us (64%)
  matrix products  23.7 us (12%)
  waiting for transfers between devices  21.9 us (11%)
  between operations  14.1 us (7%)
  other arithmetic  7.44 us (4%)
    all_gather x1, blocking collectives, body(): block_labels = lax.all_gather(labels, ('dp', 'vocab'), axis=0, tiled=True)  43.7 us
    psum x1, blocking collectives, body(): lax.psum((row_total * jnp.exp(row_top - best), target_logit), ('dp', 'voc...  40 us
    pmax x1, blocking collectives, body(): best = lax.pmax(row_top, ('dp', 'vocab'))  39.1 us
    dot_general x1, matrix products, body(): jnp.dot(block_rows, head_weight, preferred_element_type=jnp.float32)  23.7 us
    all_gather x1, waiting for transfers between devices, body(): block_rows = lax.all_gather(hidden, ('dp', 'vocab'), axis=0, tiled=True)  21.3 us
    reduce_sum x1, other arithmetic, body(): row_total = jnp.sum(jnp.exp(logits - row_top[:, None]), axis=1)  4.49 us
  transfers between devices with their start and end apart: 1, of which 1 were waited for; matrix products, arithmetic and copies ran while one was open for 1% of the time, Pallas kernels for 0%

commit v1 on v0

v1 whole, which is shorter than its diff:
```python
import functools

import jax
import jax.numpy as jnp
from jax import lax
from jax.experimental import pallas as pl
from jax.experimental.pallas import tpu as pltpu
from jax.sharding import PartitionSpec as P

BENCH = 40
AXES = ("dp", "vocab")
PARTS = 4
MESH = pl.DeviceIdType.MESH


def toggled(index, mask):
    return index + mask - 2 * mask * ((index // mask) % 2)


def runs_of(done):
    slots = [0]
    for bit in done:
        slots = slots + [slot + (1 << bit) for slot in slots]
    slots.sort()
    runs = []
    for slot in slots:
        if runs and runs[-1][0] + runs[-1][1] == slot:
            runs[-1][1] += 1
        else:
            runs.append([slot, 1])
    return runs


def kernel(
    n, vocab_size, hidden, weight, targets, bench_ids, valid, lengths,
    token_loss, bench_loss, bench_count,
    x_own, x_far, w_own, w_far, acc, labels, mine_own, mine_far, mine_lab,
    their_own, their_far, their_lab, stats, packed, gathered,
    w_sems, pair_send, pair_recv, hop_send, hop_recv, fwd_send, fwd_recv, st_send, st_recv,
):
    rows, depth = hidden.shape
    cols = weight.shape[1]
    kp = depth // (2 * PARTS)
    chips = n // 2
    bits = chips.bit_length() - 1
    total = chips * rows
    half = rows // 2
    me = lax.axis_index("dp") * vocab_size + lax.axis_index("vocab")
    core = me % 2
    chip = me // 2
    chip_bits = [(i + bits // 2) % bits for i in range(bits)]
    slot_me = sum(((chip // (1 << chip_bits[b])) % 2) * (1 << b) for b in range(bits))

    def place(index):
        return (index // vocab_size, index % vocab_size)

    partner = place(toggled(me, 1))

    def w_copy(far, j):
        which = (1 - core) if far else core
        start = pl.multiple_of((which * PARTS + j) * kp, kp)
        dst = (w_far if far else w_own).at[j]
        return pltpu.make_async_copy(weight.at[pl.ds(start, kp), :], dst, w_sems.at[int(far), j])

    order = []
    for j in range(PARTS):
        order.append((False, j))
        if j:
            order.append((True, j - 1))
    order.append((True, PARTS - 1))
    for far, j in order:
        w_copy(far, j).start()

    barrier = pltpu.get_barrier_semaphore()

    @pl.loop(1, n)
    def _(d):
        pl.semaphore_signal(barrier, inc=1, device_id=place((me + d) % n), device_id_type=MESH)

    lane = lax.broadcasted_iota(jnp.int32, (rows, rows), 1)
    sub = lax.broadcasted_iota(jnp.int32, (rows, rows), 0)
    eye = lane == sub

    def to_col(row):
        return jnp.sum(jnp.where(eye, jnp.broadcast_to(row, (rows, rows)), 0.0), axis=1, keepdims=True)

    pos = me * rows + lax.broadcasted_iota(jnp.int32, (1, rows), 1)
    live = valid[...]
    run = jnp.int32(0)
    for j in range(lengths.shape[0]):
        run = run + lengths[j]
        live = jnp.where(pos == run - 1, 0, live)
    live_row = live.astype(jnp.float32)
    live_col = to_col(live_row)
    tgt_col = to_col(targets[...].astype(jnp.float32))
    ben_col = to_col(bench_ids[...].astype(jnp.float32))
    rank_row = jnp.sum(jnp.where(sub <= lane, live_col, 0.0), axis=0, keepdims=True)
    rank_col = to_col(rank_row)
    spot_row = rank_row - 1.0 + (core * half).astype(jnp.float32)
    pick = jnp.where(sub.astype(jnp.float32) == spot_row, live_row, 0.0)
    pick_bf = pick.astype(jnp.bfloat16)
    lab_lane = lax.broadcasted_iota(jnp.int32, (rows, 128), 1)
    lab_in = jnp.where(lab_lane == 0, tgt_col, 0.0)
    lab_in = jnp.where(lab_lane == 1, ben_col, lab_in)
    lab_in = jnp.where(lab_lane == 2, live_col, lab_in)
    lab = jnp.zeros((rows, 128), jnp.float32)
    for j in range(rows):
        lab = lab + pick[:, j:j + 1] * lab_in[j:j + 1, :]
    mine_lab[...] = lab
    for j in range(PARTS):
        for far, dst in ((False, mine_own), (True, mine_far)):
            which = (1 - core) if far else core
            start = pl.multiple_of((which * PARTS + j) * kp, kp)
            dst[j] = jnp.dot(
                pick_bf, hidden[:, pl.ds(start, kp)], preferred_element_type=jnp.float32
            ).astype(jnp.bfloat16)

    pl.semaphore_wait(barrier, n - 1)

    pair = []
    for i, (src, dst) in enumerate(((mine_lab, their_lab), (mine_far, their_own), (mine_own, their_far))):
        copy = pltpu.make_async_remote_copy(
            src_ref=src, dst_ref=dst, send_sem=pair_send.at[i], recv_sem=pair_recv.at[i],
            device_id=partner, device_id_type=MESH)
        copy.start()
        pair.append(copy)
    pair[0].wait_recv()
    labels[0:rows, :] = mine_lab[...] + their_lab[...]
    pair[1].wait_recv()
    for j in range(PARTS):
        x_own[j, 0:rows, :] = mine_own[j] + their_own[j]

    count = [0]
    sends = []

    def hop(ref, bit, done):
        target = place(toggled(me, 2 << chip_bits[bit]))
        copies = []
        for start, length in runs_of(done):
            src = ref.at[pl.ds(start * rows, length * rows), :]
            dst = ref.at[pl.ds((start + (1 << bit)) * rows, length * rows), :]
            i = count[0]
            count[0] += 1
            copy = pltpu.make_async_remote_copy(
                src_ref=src, dst_ref=dst, send_sem=hop_send.at[i], recv_sem=hop_recv.at[i],
                device_id=target, device_id_type=MESH)
            copy.start()
            copies.append(copy)
        sends.extend(copies)
        return copies

    plan_a = list(range(bits))
    plan_b = plan_a[:-2] + [plan_a[-1], plan_a[-2]] if bits >= 2 else plan_a
    streams = [(labels, plan_a)] + [(x_own.at[j], plan_b if j % 2 else plan_a) for j in range(PARTS)]
    flying = [[] for _ in streams]
    for step in range(bits):
        for i, (ref, plan) in enumerate(streams):
            for copy in flying[i]:
                copy.wait_recv()
            flying[i] = hop(ref, plan[step], plan[:step])
        if step == 0:
            pair[2].wait_recv()
            for j in range(PARTS):
                x_far[j, 0:rows, :] = mine_far[j] + their_far[j]
    for copy in flying[0]:
        copy.wait_recv()

    def forward(j):
        return pltpu.make_async_remote_copy(
            src_ref=x_own.at[j, pl.ds(rows, total - rows), :],
            dst_ref=x_far.at[j, pl.ds(rows, total - rows), :],
            send_sem=fwd_send.at[j], recv_sem=fwd_recv.at[j],
            device_id=partner, device_id_type=MESH)

    width = 1024

    def multiply(far, j, first):
        w_copy(far, j).wait()
        x = (x_far if far else x_own)[j]
        w = (w_far if far else w_own).at[j]
        for start in range(0, cols, width):
            stop = min(cols, start + width)
            part = jnp.dot(x, w[:, start:stop], preferred_element_type=jnp.float32)
            if first:
                acc[:, start:stop] = part
            else:
                acc[:, start:stop] += part

    for far, j in order:
        if far:
            forward(j).wait_recv()
        else:
            for copy in flying[j + 1]:
                copy.wait_recv()
            forward(j).start()
        multiply(far, j, first=(not far and j == 0))

    block = 64
    offset = me * cols

    @pl.loop(0, total // block)
    def _(i):
        start = pl.multiple_of(i * block, block)
        lab = labels[pl.ds(start, block), :]
        ids = lab[:, 0:1].astype(jnp.int32) - offset
        values = acc[pl.ds(start, block), :]
        column = lax.broadcasted_iota(jnp.int32, (block, cols), 1)
        goal = jnp.sum(jnp.where(column == ids, values, 0.0), axis=1, keepdims=True)
        top = jnp.max(values, axis=1, keepdims=True)
        summed = jnp.sum(jnp.exp(values - top), axis=1, keepdims=True)
        at = lax.broadcasted_iota(jnp.int32, (block, 128), 1)
        out = jnp.where(at == 0, top, 0.0)
        out = jnp.where(at == 1, summed, out)
        out = jnp.where(at == 2, goal, out)
        out = jnp.where(at == 3, lab[:, 1:2], out)
        out = jnp.where(at == 4, lab[:, 2:3], out)
        for k in range(block // rows):
            slot = i * (block // rows) + k
            true_slot = sum(
                (((slot // (1 << b)) % 2 + (slot_me // (1 << b)) % 2) % 2) * (1 << b) for b in range(bits))
            stats[pl.ds(pl.multiple_of(true_slot * rows, rows), rows), :] = out[k * rows:(k + 1) * rows]

    lanes = [stats[b * 128:(b + 1) * 128, :].T for b in range(total // 128)]
    packed[...] = jnp.concatenate([t[0:4, :] for t in lanes], axis=0)
    ben_lane = [t[3:4, :] for t in lanes]
    live_lane = [t[4:5, :] for t in lanes]

    def st_copy(d):
        return pltpu.make_async_remote_copy(
            src_ref=packed, dst_ref=gathered.at[me], send_sem=st_send.at[d], recv_sem=st_recv.at[me],
            device_id=place((me + d) % n), device_id_type=MESH)

    @pl.loop(1, n)
    def _(d):
        st_copy(d).start()

    gathered[me] = packed[...]
    for copy in pair + sends + [forward(j) for j in range(PARTS)]:
        copy.wait_send()

    @pl.loop(1, n)
    def _(d):
        st_copy(d).wait_send()
        source = (me + d) % n
        pltpu.make_async_remote_copy(
            src_ref=packed, dst_ref=gathered.at[source], send_sem=st_send.at[d],
            recv_sem=st_recv.at[source], device_id=place(source), device_id_type=MESH).wait_recv()

    bench = lax.broadcasted_iota(jnp.int32, (BENCH, 128), 0).astype(jnp.float32)
    sums = jnp.zeros((BENCH, 1), jnp.float32)
    counts = jnp.zeros((BENCH, 1), jnp.float32)
    own = jnp.zeros((rows, 1), jnp.float32)
    spot = (slot_me * rows + core * half).astype(jnp.float32) + rank_col - 1.0
    for b in range(total // 128):
        tops = gathered[:, 4 * b, :]
        best = jnp.max(tops, axis=0, keepdims=True)
        summed = jnp.sum(gathered[:, 4 * b + 1, :] * jnp.exp(tops - best), axis=0, keepdims=True)
        goal = jnp.sum(gathered[:, 4 * b + 2, :], axis=0, keepdims=True)
        loss = best + jnp.log(summed) - goal
        hot = jnp.where(bench == ben_lane[b], live_lane[b], 0.0)
        sums = sums + jnp.sum(hot * loss, axis=1, keepdims=True)
        counts = counts + jnp.sum(hot, axis=1, keepdims=True)
        where = (lax.broadcasted_iota(jnp.int32, (rows, 128), 1) + b * 128).astype(jnp.float32)
        own = own + jnp.sum(jnp.where(where == spot, loss, 0.0), axis=1, keepdims=True)

    def to_row(col):
        size = col.shape[0]
        square = lax.broadcasted_iota(jnp.int32, (size, size), 0) == lax.broadcasted_iota(jnp.int32, (size, size), 1)
        return jnp.sum(jnp.where(square, col, 0.0), axis=0, keepdims=True)

    token_loss[...] = to_row(own * live_col)
    bench_loss[...] = to_row(sums / jnp.maximum(counts, 1.0))
    bench_count[...] = to_row(counts)


def body(hidden, head_weight, targets, bench_ids, valid, seq_lengths):
    n = lax.axis_size(AXES)
    vocab_size = lax.axis_size("vocab")
    rows, depth = hidden.shape
    cols = head_weight.shape[1]
    chips = n // 2
    bits = chips.bit_length() - 1
    total = chips * rows
    kp = depth // (2 * PARTS)
    hops = bits + PARTS * (bits + 1)
    bf, f32 = jnp.bfloat16, jnp.float32
    vmem = pl.BlockSpec(memory_space=pltpu.VMEM)
    dma = pltpu.SemaphoreType.DMA
    out = pl.pallas_call(
        functools.partial(kernel, n, vocab_size),
        out_shape=(
            jax.ShapeDtypeStruct((1, rows), f32),
            jax.ShapeDtypeStruct((1, BENCH), f32),
            jax.ShapeDtypeStruct((1, BENCH), f32),
        ),
        in_specs=[vmem, pl.BlockSpec(memory_space=pl.ANY), vmem, vmem, vmem,
                  pl.BlockSpec(memory_space=pltpu.SMEM)],
        out_specs=(vmem, vmem, vmem),
        scratch_shapes=[
            pltpu.VMEM((PARTS, total, kp), bf),
            pltpu.VMEM((PARTS, total, kp), bf),
            pltpu.VMEM((PARTS, kp, cols), bf),
            pltpu.VMEM((PARTS, kp, cols), bf),
            pltpu.VMEM((total, cols), f32),
            pltpu.VMEM((total, 128), f32),
            pltpu.VMEM((PARTS, rows, kp), bf),
            pltpu.VMEM((PARTS, rows, kp), bf),
            pltpu.VMEM((rows, 128), f32),
            pltpu.VMEM((PARTS, rows, kp), bf),
            pltpu.VMEM((PARTS, rows, kp), bf),
            pltpu.VMEM((rows, 128), f32),
            pltpu.VMEM((total, 128), f32),
            pltpu.VMEM((total // 32, 128), f32),
            pltpu.VMEM((n, total // 32, 128), f32),
            dma((2, PARTS)), dma((3,)), dma((3,)), dma((hops,)), dma((hops,)),
            dma((PARTS,)), dma((PARTS,)), dma((n,)), dma((n,)),
        ],
        compiler_params=pltpu.CompilerParams(
            collective_id=0, has_side_effects=True, vmem_limit_bytes=60 << 20),
    )(hidden, head_weight, targets.reshape(1, rows), bench_ids.reshape(1, rows),
      valid.reshape(1, rows), seq_lengths)
    return out[0].reshape(rows), out[1].reshape(BENCH), out[2].reshape(BENCH)


def solution(mesh):
    placed = (
        P(AXES, None),
        P(None, AXES),
        P(AXES),
        P(AXES),
        P(AXES),
        P(),
    )
    return jax.shard_map(
        body, mesh=mesh, in_specs=placed, out_specs=(P(AXES), P(), P()), check_vma=False
    )
```

time: 191 us -> 93 us (0.49)
  blocking collectives: 123 us -> 0 us
  Pallas kernels: 0 us -> 46.4 us
  local copies, waits for them, and re-layouts: 0.84 us -> 44.8 us
  matrix products: 23.7 us -> 0 us
  waiting for transfers between devices: 21.9 us -> 0 us
  between operations: 14.1 us -> 0.64 us
  other arithmetic: 7.44 us -> 0 us
    pallas_call x0 -> x1, Pallas kernels: none -> 46.4 us  [body(): pl.pallas_call(functools.partial(kernel, n, vocab_size), out_shape=(jax.S...]
    unnamed x5 -> x4, local copies, waits for them, and re-layouts: 0.1 us -> 44.8 us
    all_gather x1 -> x0, blocking collectives: 43.7 us -> none  [body(): block_labels = lax.all_gather(labels, ('dp', 'vocab'), axis=0, tiled=True)]
    psum x1 -> x0, blocking collectives: 40 us -> none  [body(): lax.psum((row_total * jnp.exp(row_top - best), target_logit), ('dp', 'voc...]
    pmax x1 -> x0, blocking collectives: 39.1 us -> none  [body(): best = lax.pmax(row_top, ('dp', 'vocab'))]
    dot_general x1 -> x0, matrix products: 23.7 us -> none  [body(): jnp.dot(block_rows, head_weight, preferred_element_type=jnp.float32)]
    all_gather x1 -> x0, waiting for transfers between devices: 21.3 us -> none  [body(): block_rows = lax.all_gather(hidden, ('dp', 'vocab'), axis=0, tiled=True)]
    reduce_sum x2 -> x0, other arithmetic: 4.61 us -> none  [the longest x1 4.49 us: body(): row_total = jnp.sum(jnp.exp(logits - row_top[:, None]), axis=1)]
  transfers between devices with their start and end apart: 1 -> 0, of which waited for: 1 -> 0; matrix products, arithmetic and copies ran while one was open for 1% -> 0% of each run, Pallas kernels for 0% -> 0%
where the time goes in v1:
time: 93 us; the launch traced here: 91.8 us
  Pallas kernels  46.4 us (50%)
  local copies, waits for them, and re-layouts  44.8 us (48%)
    pallas_call x1, Pallas kernels, body(): pl.pallas_call(functools.partial(kernel, n, vocab_size), out_shape=(jax.S...  46.4 us
    unnamed x4, local copies, waits for them, and re-layouts  44.8 us

profile of v1, /device:TPU:0, one launch (start us, length us, event | category | flops | bytes accessed | tf_op | source)
XLA Modules:
  0.0 91.8 jit_solution(5258707176514806047)
XLA Ops:
  0.6 41.3 %copy.9.weight = bf16[4096,4008]{1,0:T(8,128)(2,1)} copy(bf16[4096,4008]{0,1:T(8,128)(2,1)} %param.7) | data formatting | bytes 65667072 | tf_op args[1]
  41.9 46.4 %shard_map.85 = (f32[1,16]{1,0:T(1,128)}, f32[1,40]{1,0:T(1,128)}, f32[1,40]{1,0:T(1,128)}) custom-call(bf16[16,4096]{1,0:T(8,128)(2,1)} %hidden.1, bf16[4096,4008]{1,0:T(8,128)(2,1)} %copy.9.weight, s32[1,16]{1,0:T(1,128)} %bitcast.6, s32[1,16]{1,0:T(1,128)} %bitcast.7, s32[1,16]{1,0:T(1,128)} %bitcast.8, s32[16]{0:T(128)} %lengths.1), custom_call_target="tpu_custom_call" | custom-call | tf_op jit(solution)/shard_map/pallas_call | solution.py:289
  88.3 1.1 %copy.13 = f32[16]{0:T(128)} copy(f32[16]{0:T(128)} %bitcast.11) | data formatting | bytes 128
  89.4 1.2 %copy.14 = f32[40]{0:T(128)} copy(f32[40]{0:T(128)} %bitcast.10) | data formatting | bytes 320
  90.6 1.2 %copy.15 = f32[40]{0:T(128)} copy(f32[40]{0:T(128)} %bitcast.9) | data formatting | bytes 320

commit v2 on v1

--- a/solution.py
+++ b/solution.py
@@ -33,13 +33,13 @@
 
 def kernel(
     n, vocab_size, hidden, weight, targets, bench_ids, valid, lengths,
-    token_loss, bench_loss, bench_count,
+    result,
     x_own, x_far, w_own, w_far, acc, labels, mine_own, mine_far, mine_lab,
     their_own, their_far, their_lab, stats, packed, gathered,
     w_sems, pair_send, pair_recv, hop_send, hop_recv, fwd_send, fwd_recv, st_send, st_recv,
 ):
     rows, depth = hidden.shape
-    cols = weight.shape[1]
+    cols = weight.shape[0]
     kp = depth // (2 * PARTS)
     chips = n // 2
     bits = chips.bit_length() - 1
@@ -60,7 +60,7 @@
         which = (1 - core) if far else core
         start = pl.multiple_of((which * PARTS + j) * kp, kp)
         dst = (w_far if far else w_own).at[j]
-        return pltpu.make_async_copy(weight.at[pl.ds(start, kp), :], dst, w_sems.at[int(far), j])
+        return pltpu.make_async_copy(weight.at[:, pl.ds(start, kp)], dst, w_sems.at[int(far), j])
 
     order = []
     for j in range(PARTS):
@@ -180,11 +180,12 @@
         w = (w_far if far else w_own).at[j]
         for start in range(0, cols, width):
             stop = min(cols, start + width)
-            part = jnp.dot(x, w[:, start:stop], preferred_element_type=jnp.float32)
+            part = lax.dot_general(
+                w[start:stop, :], x, (((1,), (1,)), ((), ())), preferred_element_type=jnp.float32)
             if first:
-                acc[:, start:stop] = part
+                acc[start:stop, :] = part
             else:
-                acc[:, start:stop] += part
+                acc[start:stop, :] += part
 
     for far, j in order:
         if far:
@@ -195,29 +196,57 @@
             forward(j).start()
         multiply(far, j, first=(not far and j == 0))
 
-    block = 64
     offset = me * cols
-
-    @pl.loop(0, total // block)
-    def _(i):
-        start = pl.multiple_of(i * block, block)
-        lab = labels[pl.ds(start, block), :]
-        ids = lab[:, 0:1].astype(jnp.int32) - offset
-        values = acc[pl.ds(start, block), :]
-        column = lax.broadcasted_iota(jnp.int32, (block, cols), 1)
-        goal = jnp.sum(jnp.where(column == ids, values, 0.0), axis=1, keepdims=True)
-        top = jnp.max(values, axis=1, keepdims=True)
-        summed = jnp.sum(jnp.exp(values - top), axis=1, keepdims=True)
-        at = lax.broadcasted_iota(jnp.int32, (block, 128), 1)
-        out = jnp.where(at == 0, top, 0.0)
-        out = jnp.where(at == 1, summed, out)
-        out = jnp.where(at == 2, goal, out)
-        out = jnp.where(at == 3, lab[:, 1:2], out)
+    label_lanes = [labels[b * 128:(b + 1) * 128, :].T for b in range(total // 128)]
+    ids = jnp.concatenate([t[0:1, :] for t in label_lanes], axis=1).astype(jnp.int32) - offset
+    block = 128
+    full = cols // block
+    tail = cols - full * block
+
+    def fold(values, op):
+        size = values.shape[0]
+        whole = size // 8 * 8
+        out = op(values[:whole].reshape(whole // 8, 8, total), axis=0)
+        return op(out, axis=0, keepdims=True), values[whole:]
+
+    def scan(op, merge, init, make):
+        def reduced(values):
+            out, rest = fold(values, op)
+            return merge(out, op(rest, axis=0, keepdims=True)) if rest.shape[0] else out
+
+        def wide(i, carry):
+            values = make(pl.multiple_of(i * block, block), block)
+            return merge(carry, op(values.reshape(block // 8, 8, total), axis=0))
+
+        carry = lax.fori_loop(0, full, wide, jnp.full((8, total), init, jnp.float32))
+        out = op(carry, axis=0, keepdims=True)
+        if tail:
+            out = merge(out, reduced(make(full * block, tail)))
+        return out
+
+    def load(start, size):
+        return acc[pl.ds(start, size), :]
+
+    top = scan(jnp.max, jnp.maximum, -jnp.inf, load)
+    summed = scan(jnp.sum, jnp.add, 0.0, lambda start, size: jnp.exp(load(start, size) - top))
+
+    def hits(start, size):
+        row = lax.broadcasted_iota(jnp.int32, (size, total), 0) + start
+        return jnp.where(row == ids, load(start, size), 0.0)
+
+    goal = scan(jnp.sum, jnp.add, 0.0, hits)
+    at = lax.broadcasted_iota(jnp.int32, (128, 128), 1)
+    for b in range(total // 128):
+        part = slice(b * 128, (b + 1) * 128)
+        rest = jnp.zeros((125, 128), jnp.float32)
+        cols_of = jnp.concatenate([top[:, part], summed[:, part], goal[:, part], rest], axis=0).T
+        lab = labels[part, :]
+        out = jnp.where(at == 3, lab[:, 1:2], cols_of)
         out = jnp.where(at == 4, lab[:, 2:3], out)
-        for k in range(block // rows):
-            slot = i * (block // rows) + k
+        for k in range(128 // rows):
+            slot = b * (128 // rows) + k
             true_slot = sum(
-                (((slot // (1 << b)) % 2 + (slot_me // (1 << b)) % 2) % 2) * (1 << b) for b in range(bits))
+                (((slot // (1 << c)) % 2 + (slot_me // (1 << c)) % 2) % 2) * (1 << c) for c in range(bits))
             stats[pl.ds(pl.multiple_of(true_slot * rows, rows), rows), :] = out[k * rows:(k + 1) * rows]
 
     lanes = [stats[b * 128:(b + 1) * 128, :].T for b in range(total // 128)]
@@ -268,9 +297,10 @@
         square = lax.broadcasted_iota(jnp.int32, (size, size), 0) == lax.broadcasted_iota(jnp.int32, (size, size), 1)
         return jnp.sum(jnp.where(square, col, 0.0), axis=0, keepdims=True)
 
-    token_loss[...] = to_row(own * live_col)
-    bench_loss[...] = to_row(sums / jnp.maximum(counts, 1.0))
-    bench_count[...] = to_row(counts)
+    result[...] = jnp.zeros(result.shape, jnp.float32)
+    result[0:1, 0:rows] = to_row(own * live_col)
+    result[1:2, 0:BENCH] = to_row(sums)
+    result[2:3, 0:BENCH] = to_row(counts)
 
 
 def body(hidden, head_weight, targets, bench_ids, valid, seq_lengths):
@@ -288,20 +318,16 @@
     dma = pltpu.SemaphoreType.DMA
     out = pl.pallas_call(
         functools.partial(kernel, n, vocab_size),
-        out_shape=(
-            jax.ShapeDtypeStruct((1, rows), f32),
-            jax.ShapeDtypeStruct((1, BENCH), f32),
-            jax.ShapeDtypeStruct((1, BENCH), f32),
-        ),
+        out_shape=jax.ShapeDtypeStruct((8, 128), f32),
         in_specs=[vmem, pl.BlockSpec(memory_space=pl.ANY), vmem, vmem, vmem,
                   pl.BlockSpec(memory_space=pltpu.SMEM)],
-        out_specs=(vmem, vmem, vmem),
+        out_specs=vmem,
         scratch_shapes=[
             pltpu.VMEM((PARTS, total, kp), bf),
             pltpu.VMEM((PARTS, total, kp), bf),
-            pltpu.VMEM((PARTS, kp, cols), bf),
-            pltpu.VMEM((PARTS, kp, cols), bf),
-            pltpu.VMEM((total, cols), f32),
+            pltpu.VMEM((PARTS, cols, kp), bf),
+            pltpu.VMEM((PARTS, cols, kp), bf),
+            pltpu.VMEM((cols, total), f32),
             pltpu.VMEM((total, 128), f32),
             pltpu.VMEM((PARTS, rows, kp), bf),
             pltpu.VMEM((PARTS, rows, kp), bf),
@@ -317,9 +343,10 @@
         ],
         compiler_params=pltpu.CompilerParams(
             collective_id=0, has_side_effects=True, vmem_limit_bytes=60 << 20),
-    )(hidden, head_weight, targets.reshape(1, rows), bench_ids.reshape(1, rows),
+    )(hidden, head_weight.T, targets.reshape(1, rows), bench_ids.reshape(1, rows),
       valid.reshape(1, rows), seq_lengths)
-    return out[0].reshape(rows), out[1].reshape(BENCH), out[2].reshape(BENCH)
+    counts = out[2, :BENCH]
+    return out[0, :rows], out[1, :BENCH] / jnp.maximum(counts, 1.0), counts
 
 
 def solution(mesh):

time: 93 us -> 50.4 us (0.54)
  local copies, waits for them, and re-layouts: 44.8 us -> 1.18 us
  other arithmetic: 0 us -> 1.27 us
    unnamed x4 -> x0, local copies, waits for them, and re-layouts: 44.8 us -> none
    div x0 -> x1, other arithmetic: none -> 1.27 us  [body(): return (out[0, :rows], out[1, :BENCH] / jnp.maximum(counts, 1.0), counts)]
    squeeze x0 -> x1, local copies, waits for them, and re-layouts: none -> 1.18 us  [body(): return (out[0, :rows], out[1, :BENCH] / jnp.maximum(counts, 1.0), counts)]
where the time goes in v2:
time: 50.4 us; the launch traced here: 50.1 us
  Pallas kernels  47 us (93%)
  other arithmetic  1.27 us (3%)
  local copies, waits for them, and re-layouts  1.18 us (2%)
  between operations  0.64 us (1%)
    pallas_call x1, Pallas kernels, body(): pl.pallas_call(functools.partial(kernel, n, vocab_size), out_shape=jax.Sh...  47 us
    div x1, other arithmetic, body(): return (out[0, :rows], out[1, :BENCH] / jnp.maximum(counts, 1.0), counts)  1.27 us
    squeeze x1, local copies, waits for them, and re-layouts, body(): return (out[0, :rows], out[1, :BENCH] / jnp.maximum(counts, 1.0), counts)  1.18 us

profile of v2, /device:TPU:0, one launch (start us, length us, event | category | flops | bytes accessed | tf_op | source)
XLA Modules:
  0.0 50.1 jit_solution(17702097220794608517)
XLA Ops:
  0.6 47.0 %shard_map.85 = f32[8,128]{1,0:T(8,128)} custom-call(bf16[16,4096]{1,0:T(8,128)(2,1)} %hidden.1, bf16[4008,4096]{1,0:T(8,128)(2,1)} %bitcast.11, s32[1,16]{1,0:T(1,128)} %bitcast.12, s32[1,16]{1,0:T(1,128)} %bitcast.13, s32[1,16]{1,0:T(1,128)} %bitcast.14, s32[16]{0:T(128)} %lengths.1), custom_call_target="tpu_custom_call" | custom-call | tf_op jit(solution)/shard_map/pallas_call | solution.py:319
  47.7 1.3 %bitcast_divide_fusion = (f32[40]{0:T(128)}, f32[40]{0:T(128)}) fusion(f32[8,128]{1,0:T(8,128)} %shard_map.85), kind=kLoop, calls=%fused_computation | loop fusion | flops 80 | bytes 640 | tf_op jit(solution)/shard_map/div | solution.py:349
  48.9 1.2 %slice_bitcast_fusion.1 = f32[16]{0:T(128)} fusion(f32[8,128]{1,0:T(8,128)} %shard_map.85), kind=kLoop, calls=%fused_computation.2 | loop fusion | bytes 128 | tf_op jit(solution)/shard_map/squeeze | solution.py:349
